TPU v7x, 32 devices: a whole 2x2x4 slice. The times are simulated.
32 devices in a mesh: dp: 4 (over y, x), vocab: 8 (over z, core).
Axes of the slice: x: 2, y: 2, z: 4, core: 2. Of those that a mesh axis runs over, the one named last changes fastest.
Arguments:
- hidden: bfloat16 [512, 8192], P('dp', 'vocab'), may hold values from -20 to 20
- weight: bfloat16 [8192, 4752], P('dp', 'vocab'), may hold values from -0.198873782 to 0.198873782
- targets: int32 [512], P('dp'), may hold values from 0 to 4751
- loss_mask: int32 [512], P('dp'), may hold values 0 or 1
Outputs:
- grad_hidden: bfloat16 [512, 8192], P('dp', 'vocab')
- grad_weight: bfloat16 [8192, 4752], P('dp', 'vocab')
- token_loss: float32 [512], P('dp')
- grad_norm: float32 [], replicated
All inputs are finite; a program needn't handle non-finite values. No bound on the sum of `loss_mask` on one device may be relied on, other than what follows from the above.
Results may differ from a plain program's by a relative error of at most 0.0034.
Values may be sent and summed in bfloat16 or wider, within the bound.
A program may use at most 128 MiB of HBM per device.

v0:
```python
import functools

import jax
import jax.numpy as jnp
from jax import lax
from jax.experimental import pallas as pl
from jax.experimental.pallas import tpu as pltpu
from jax.sharding import PartitionSpec as P

loss_scale = 16.0
MESH = pl.DeviceIdType.MESH
f32 = jnp.float32
bf16 = jnp.bfloat16


def dot_nn(a, b):
    return jnp.dot(a, b, preferred_element_type=f32)


def dot_nt(a, b):
    return lax.dot_general(a, b, (((1,), (1,)), ((), ())), preferred_element_type=f32)


def dot_tn(a, b):
    return lax.dot_general(a, b, (((0,), (0,)), ((), ())), preferred_element_type=f32)


def kernel(
    n, nv, cpc, nc, ng,
    hid, w_in, tgt, keep,
    hg_out, wg_out, loss_out, norm_out,
    w, wg, gat, hb, lp, lr, st, sr, dall, ps, pr, gs, g1, g2, n1s, n1, n2s, n2,
    h1_s, h1_r, h2_s, hb_r, h3_s, l_s, l_r, s_s, s_r, d_s, d_r,
    io, p_s, p_r, g1_s, g1_r, g2_s, g2_r, n1_s, n1_r, n2_s, n2_r,
):
    T, F = hid.shape
    V = w.shape[0]
    Tc, Tg = T // nc, T // ng
    bpd = nv // n
    zpd = bpd // cpc
    nz = nv // cpc
    k = lax.axis_index("dp")
    j = lax.axis_index("vocab")
    z, c = j // cpc, j % cpc
    sends = []

    def push(src, dst, ss, rs, dp, vocab):
        copy = pltpu.make_async_remote_copy(
            src_ref=src, dst_ref=dst, send_sem=ss, recv_sem=rs,
            device_id={"dp": dp, "vocab": vocab}, device_id_type=MESH,
        )
        copy.start()
        sends.append((src, ss))

    def local(src, dst, sem):
        pltpu.make_async_copy(src, dst, sem).start()

    def arrived(dst, sem):
        pltpu.make_async_copy(dst, dst, sem).wait()

    def turn(s, base, size):
        return lax.rem(base + s, size)

    def columns(q, core):
        if F % 128 == 0:
            return w[:, pl.ds(pl.multiple_of((q * cpc + core) * F, F), F)]
        out = w[:, q * cpc * F:(q * cpc + 1) * F]
        for a in range(1, cpc):
            out = jnp.where(core == a, w[:, (q * cpc + a) * F:(q * cpc + a + 1) * F], out)
        return out

    row_order = list(range(1, n)) + [0]

    weight_in = pltpu.make_async_copy(w_in, w, io.at[0])
    weight_in.start()

    barrier = pltpu.get_barrier_semaphore()
    for s in range(1, nv):
        pl.semaphore_signal(barrier, inc=1, device_id={"dp": k, "vocab": turn(s, j, nv)}, device_id_type=MESH)
    for s in range(1, n):
        pl.semaphore_signal(barrier, inc=1, device_id={"dp": turn(s, k, n), "vocab": j}, device_id_type=MESH)
    pl.semaphore_wait(barrier, nv + n - 2)

    for h in range(nc):
        piece = hid.at[pl.ds(h * Tc, Tc)]
        for s in range(1, nz):
            to = turn(s, z, nz)
            push(piece, gat.at[z, h], h1_s.at[s, h], h1_r.at[z, h], k, to * cpc + c)
        local(piece, gat.at[z, h], h1_r.at[z, h])

    def exchange(h):
        for s in row_order:
            i = turn(s, k, n)
            for q in range(zpd):
                src = gat.at[i * zpd + q, h]
                arrived(src, h1_r.at[i * zpd + q, h])
                bl = q * cpc + c
                if s:
                    push(src, hb.at[bl, h, k], h2_s.at[s, q, h], hb_r.at[k, bl, h], i, j)
                else:
                    local(src, hb.at[bl, h, k], hb_r.at[k, bl, h])

    def partial(h):
        for s in [0] + list(range(1, n)):
            t = turn(s, k, n)
            for q in range(zpd):
                bl = q * cpc + c
                slot = hb.at[bl, h, t]
                arrived(slot, hb_r.at[t, bl, h])
                for d in range(1, cpc):
                    push(slot, slot, h3_s.at[s, q, d, h], hb_r.at[t, bl, h], k, z * cpc + turn(d, c, cpc))
        for s in [0] + list(range(1, n)):
            t = turn(s, k, n)
            for q in range(zpd):
                for d in range(1, cpc):
                    bl = q * cpc + turn(d, c, cpc)
                    arrived(hb.at[bl, h, t], hb_r.at[t, bl, h])
        total = dot_nt(hb[0, h].reshape(n * Tc, F), w[:, 0:F])
        for bl in range(1, bpd):
            total += dot_nt(hb[bl, h].reshape(n * Tc, F), w[:, bl * F:(bl + 1) * F])
        lp[h] = total.reshape(n, Tc, V)
        for s in range(1, n):
            t = turn(s, k, n)
            push(lp.at[h, t], lr.at[h, s - 1], l_s.at[s - 1, h], l_r.at[s - 1, h], t, j)

    exchange(0)
    weight_in.wait()
    for h in range(nc):
        if h + 1 < nc:
            exchange(h + 1)
        partial(h)
    rows = []
    for h in range(nc):
        own = lp[h, k]
        for s in range(n - 1):
            arrived(lr.at[h, s], l_r.at[s, h])
            own += lr[h, s]
        rows.append(own)
    logits = jnp.concatenate(rows, axis=0)

    def to_column(row):
        return jnp.transpose(jnp.broadcast_to(row, (128, T)))[:, :1]

    target_col = to_column(tgt[...].astype(f32)).astype(jnp.int32) - j * V
    onehot = lax.broadcasted_iota(jnp.int32, (T, V), 1) == target_col
    top = jnp.max(logits, axis=1, keepdims=True)
    part = jnp.sum(jnp.exp(logits - top), axis=1, keepdims=True)
    hit = jnp.sum(jnp.where(onehot, logits, 0.0), axis=1, keepdims=True)
    lane = lax.broadcasted_iota(jnp.int32, (T, 128), 1)
    packed = jnp.where(lane == 0, top, jnp.where(lane == 1, part, hit))
    mine = jnp.transpose(packed)[:8, :]
    st[...] = mine
    sr[j] = mine
    for s in range(1, nv):
        push(st, sr.at[j], s_s.at[s], s_r.at[j], k, turn(s, j, nv))
    for s in range(1, nv):
        frm = turn(s, j, nv)
        arrived(sr.at[frm], s_r.at[frm])
    stats = sr[...]
    tops, parts, hits = stats[:, 0, :], stats[:, 1, :], stats[:, 2, :]
    row_top = jnp.max(tops, axis=0, keepdims=True)
    exp_sum = jnp.sum(parts * jnp.exp(tops - row_top), axis=0, keepdims=True)
    target_logit = jnp.sum(hits, axis=0, keepdims=True)
    log_total = row_top + jnp.log(exp_sum)
    row_keep = keep[...].astype(f32)
    loss_out[...] = row_keep * (log_total - target_logit)

    soft = jnp.exp(logits - to_column(log_total))
    dl = (loss_scale * to_column(row_keep) * (soft - jnp.where(onehot, 1.0, 0.0))).astype(bf16)
    dall[:, k] = dl.reshape(nc, Tc, V)

    shift = [0] + [1 + lax.rem(z + m, n - 1) for m in range(n - 1)]

    def ahead(s):
        return turn(shift[s], k, n)

    def behind(s):
        return turn(n - shift[s], k, n)

    for s in range(1, n):
        push(dall.at[:, k], dall.at[:, k], d_s.at[s], d_r.at[k], behind(s), j)

    def other_part(s):
        t = ahead(s)
        if s:
            arrived(dall.at[:, t], d_r.at[t])
        rows = dall[:, t].reshape(T, V)
        for d in range(1, cpc):
            other = turn(d, c, cpc)
            for q in range(zpd):
                ps[s, d - 1, q] = dot_nn(rows, columns(q, other))
            push(ps.at[s, d - 1], pr.at[s, d - 1], p_s.at[s, d - 1], p_r.at[s, d - 1], k, z * cpc + other)

    def relay(s, src, q, g):
        to = behind(s) * zpd + q
        dst = g2.at[z, pl.ds(g * Tg, Tg)]

        @pl.when(to != z)
        def _():
            pltpu.make_async_remote_copy(
                src_ref=src, dst_ref=dst, send_sem=g2_s.at[s, q, g], recv_sem=g2_r.at[z, g],
                device_id={"dp": k, "vocab": to * cpc + c}, device_id_type=MESH,
            ).start()

        @pl.when(to == z)
        def _():
            pltpu.make_async_copy(src, dst, g2_r.at[z, g]).start()

    def own_part(s):
        t = ahead(s)
        rows = dall[:, t].reshape(T, V)
        for d in range(1, cpc):
            arrived(pr.at[s, d - 1], p_r.at[s, d - 1])
        for q in range(zpd):
            part_sum = dot_nn(rows, columns(q, c))
            for d in range(1, cpc):
                part_sum += pr[s, d - 1, q]
            gs[s, q] = part_sum.astype(bf16)
        for g in range(ng):
            if s:
                piece = gs.at[s, :, pl.ds(g * Tg, Tg)]
                push(piece, g1.at[k, :, pl.ds(g * Tg, Tg)], g1_s.at[s, g], g1_r.at[k, g], t, j)
            else:
                for q in range(zpd):
                    relay(0, gs.at[0, q, pl.ds(g * Tg, Tg)], q, g)

    other_part(0)
    own_part(0)
    for s in range(1, n):
        other_part(s)
        if s > 1:
            own_part(s - 1)
    own_part(n - 1)

    grads = jnp.transpose(dall[...].reshape(n * T, V))
    squares = jnp.zeros((1, F), f32)
    per = -(-bpd // n)
    done = 0
    for s in range(1, n + 1):
        for bl in range(done, min(done + per, bpd)):
            grad = dot_nn(grads, hb[bl].reshape(n * T, F))
            wg[:, bl * F:(bl + 1) * F] = grad.astype(bf16)
            squares += jnp.sum(grad * grad, axis=0, keepdims=True)
        done += per
        if s < n:
            i = behind(s)
            for g in range(ng):
                arrived(g1.at[i, :, pl.ds(g * Tg, Tg)], g1_r.at[i, g])
                for q in range(zpd):
                    relay(s, g1.at[i, q, pl.ds(g * Tg, Tg)], q, g)
    weight_out = pltpu.make_async_copy(wg, wg_out, io.at[1])
    weight_out.start()

    total = None
    for src in range(nz):
        for g in range(ng):
            arrived(g2.at[src, pl.ds(g * Tg, Tg)], g2_r.at[src, g])
        term = g2[src].astype(f32)
        total = term if total is None else total + term
    hg_out[...] = total.astype(bf16)

    both = jnp.sum(squares) + jnp.sum(total * total)
    value = jnp.full((8, 128), both, f32)
    n1s[...] = value
    n1[j] = value
    for s in range(1, nv):
        push(n1s, n1.at[j], n1_s.at[s], n1_r.at[j], k, turn(s, j, nv))
    for s in range(1, nv):
        frm = turn(s, j, nv)
        arrived(n1.at[frm], n1_r.at[frm])
    value = n1[0]
    for a in range(1, nv):
        value = value + n1[a]
    n2s[...] = value
    n2[k] = value
    for s in range(1, n):
        push(n2s, n2.at[k], n2_s.at[s], n2_r.at[k], turn(s, k, n), j)
    for s in range(1, n):
        frm = turn(s, k, n)
        arrived(n2.at[frm], n2_r.at[frm])
    value = n2[0]
    for a in range(1, n):
        value = value + n2[a]
    norm_out[...] = jnp.sqrt(value)

    for src, ss in sends:
        pltpu.make_async_copy(src, src, ss).wait()
    for s in range(n):
        i = behind(s)
        for q in range(zpd):
            @pl.when(i * zpd + q != z)
            def _():
                for g in range(ng):
                    piece = g2.at[0, pl.ds(0, Tg)]
                    pltpu.make_async_copy(piece, piece, g2_s.at[s, q, g]).wait()
    weight_out.wait()


def on_device(n, nv, hidden, weight, targets, loss_mask):
    T, F = hidden.shape
    R, V = weight.shape
    bpd = nv // n
    cpc = 2 if bpd % 2 == 0 else 1
    zpd, nz = bpd // cpc, nv // cpc
    nc = 4 if T % 64 == 0 else 1
    ng = 2 if T % 32 == 0 else 1
    dma = pltpu.SemaphoreType.DMA
    vmem = pl.BlockSpec(memory_space=pltpu.VMEM)
    hbm = pl.BlockSpec(memory_space=pl.ANY)
    others = max(cpc - 1, 1)
    hg, wg, loss, norm = pl.pallas_call(
        functools.partial(kernel, n, nv, cpc, nc, ng),
        out_shape=(
            jax.ShapeDtypeStruct((T, F), bf16),
            jax.ShapeDtypeStruct((V, R), bf16),
            jax.ShapeDtypeStruct((1, T), f32),
            jax.ShapeDtypeStruct((8, 128), f32),
        ),
        in_specs=[vmem, hbm, vmem, vmem],
        out_specs=(vmem, hbm, vmem, vmem),
        scratch_shapes=[
            pltpu.VMEM((V, R), bf16),
            pltpu.VMEM((V, R), bf16),
            pltpu.VMEM((nz, nc, T // nc, F), bf16),
            pltpu.VMEM((bpd, nc, n, T // nc, F), bf16),
            pltpu.VMEM((nc, n, T // nc, V), f32),
            pltpu.VMEM((nc, n - 1, T // nc, V), f32),
            pltpu.VMEM((8, T), f32),
            pltpu.VMEM((nv, 8, T), f32),
            pltpu.VMEM((nc, n, T // nc, V), bf16),
            pltpu.VMEM((n, others, zpd, T, F), f32),
            pltpu.VMEM((n, others, zpd, T, F), f32),
            pltpu.VMEM((n, zpd, T, F), bf16),
            pltpu.VMEM((n, zpd, T, F), bf16),
            pltpu.VMEM((nz, T, F), bf16),
            pltpu.VMEM((8, 128), f32),
            pltpu.VMEM((nv, 8, 128), f32),
            pltpu.VMEM((8, 128), f32),
            pltpu.VMEM((n, 8, 128), f32),
            dma((nz, nc)), dma((nz, nc)),
            dma((n, zpd, nc)), dma((n, bpd, nc)), dma((n, zpd, cpc, nc)),
            dma((n, nc)), dma((n, nc)),
            dma((nv,)), dma((nv,)),
            dma((n,)), dma((n,)),
            dma((2,)),
            dma((n, others)), dma((n, others)),
            dma((n, ng)), dma((n, ng)),
            dma((n, zpd, ng)), dma((nz, ng)),
            dma((nv,)), dma((nv,)),
            dma((n,)), dma((n,)),
        ],
        compiler_params=pltpu.CompilerParams(
            collective_id=0, has_side_effects=True, vmem_limit_bytes=60 * 1024 * 1024
        ),
    )(hidden, weight.T, targets.reshape(1, T), loss_mask.reshape(1, T))
    return hg, wg.T, loss.reshape(T), norm[0, 0]


def solution(mesh):
    placed = (P("dp", "vocab"), P("dp", "vocab"), P("dp"), P("dp"))
    return jax.shard_map(
        functools.partial(on_device, mesh.shape["dp"], mesh.shape["vocab"]),
        mesh=mesh,
        in_specs=placed,
        out_specs=(P("dp", "vocab"), P("dp", "vocab"), P("dp"), P()),
        check_vma=False,
    )
```

profile of v0, /device:TPU:0, one launch (start us, length us, event | category | flops | bytes accessed | tf_op | source)
XLA Modules:
  0.0 113.9 jit_solution(15743347044598756576)
XLA Ops:
  0.6 106.5 %shard_map.75 = (bf16[128,1024]{1,0:T(8,128)(2,1)}, bf16[594,2048]{1,0:T(8,128)(2,1)}, f32[1,128]{1,0:T(1,128)}, f32[8,128]{1,0:T(8,128)}) custom-call(bf16[128,1024]{1,0:T(8,128)(2,1)} %hid.1, bf16[594,2048]{1,0:T(8,128)(2,1)} %bitcast.6, s32[1,128]{1,0:T(1,128)} %bitcast.8, s32[1,128]{1,0:T(1,128)} %bitcast.9), custom_call_target="tpu_custom_call" | custom-call | tf_op jit(solution)/shard_map/pallas_call | solution.py:311
  107.1 1.2 %slice.3 = f32[1,1]{1,0:T(1,128)} slice(f32[8,128]{1,0:T(8,128)} %get-tuple-element.11), slice={[0:1], [0:1]} | slice | bytes 8 | tf_op jit(solution)/shard_map/slice | solution.py:356
  108.3 1.7 %copy.11 = bf16[128,1024]{1,0:T(8,128)(2,1)} copy(bf16[128,1024]{1,0:T(8,128)(2,1)} %get-tuple-element.16) | data formatting | bytes 524288
  109.9 0.0 copy-start
  110.0 3.4 %copy.12 = bf16[2048,594]{0,1:T(8,128)(2,1)} copy(bf16[2048,594]{0,1:T(8,128)(2,1)} %bitcast.7) | data formatting | bytes 4866048
  113.4 0.0 copy-done
  113.4 0.5 copy.13
Async XLA Ops:
  109.9 3.4 %copy-start = (f32[1,128]{1,0:T(1,128)S(1)}, f32[1,128]{1,0:T(1,128)}, u32[]{:S(2)}) copy-start(f32[1,128]{1,0:T(1,128)} %get-tuple-element.10) | copy-start | bytes 1540
where the time goes:
time: 114 us
  Pallas kernels  106 us (93%)
  local copies, waits for them, and re-layouts  6.81 us (6%)
    pallas_call x1, Pallas kernels, on_device(): pl.pallas_call(functools.partial(kernel, n, nv, cpc, nc, ng), out_shape=(...  106 us
    unnamed x5, local copies, waits for them, and re-layouts  5.62 us

commit v1 on v0

v1 whole, which is shorter than its diff:
```python
import functools

import jax
import jax.numpy as jnp
from jax import lax
from jax.experimental import pallas as pl
from jax.experimental.pallas import tpu as pltpu
from jax.sharding import PartitionSpec as P

loss_scale = 16.0
MESH = pl.DeviceIdType.MESH
f32 = jnp.float32
bf16 = jnp.bfloat16
vmem_bytes = 67043328


def dot_nn(a, b):
    return jnp.dot(a, b, preferred_element_type=f32)


def dot_nt(a, b):
    return lax.dot_general(a, b, (((1,), (1,)), ((), ())), preferred_element_type=f32)


def each(count, body):
    if count <= 32:
        for s in range(count):
            body(s)
    else:

        def step(s, carry):
            body(s)
            return carry

        lax.fori_loop(0, count, step, 0)


def kernel(
    n, nv, cpc, nc,
    hid_in, w_in, tgt_in, keep_in,
    hg_out, wg_out, loss_out, norm_out,
    hid, tgt, keep, w, gat, hb, lp, lr, lg, tcol, kcol, st, sr, dall, ps, pr, gs, g1, g2, via, mid, n1,
    io, h1_s, h1_r, h2_s, h2_r, h3_s, h3_r, l_s, l_r, s_s, s_r, d_s, d_r,
    p_s, p_r, g1_s, g1_r, g2_s, g2_r, g3_r, via_r, n_s, n_r,
):
    T, F = hid.shape
    V = w.shape[0]
    Tc = T // nc
    bpd = nv // n
    zpd = bpd // cpc
    nz = nv // cpc
    k = lax.axis_index("dp")
    j = lax.axis_index("vocab")
    z, c = j // cpc, j % cpc

    def push(src, dst, ss, rs, dp, vocab):
        pltpu.make_async_remote_copy(
            src_ref=src, dst_ref=dst, send_sem=ss, recv_sem=rs,
            device_id={"dp": dp, "vocab": vocab}, device_id_type=MESH,
        ).start()

    def arrived(dst, sem):
        pltpu.make_async_copy(dst, dst, sem).wait()

    def turn(s, base, size):
        return lax.rem(base + s, size)

    def columns(q, core):
        if F % 128 == 0:
            return w[:, pl.ds(pl.multiple_of((q * cpc + core) * F, F), F)]
        out = w[:, q * cpc * F:(q * cpc + 1) * F]
        for a in range(1, cpc):
            out = jnp.where(core == a, w[:, (q * cpc + a) * F:(q * cpc + a + 1) * F], out)
        return out

    def to_wide(row):
        return jnp.transpose(jnp.broadcast_to(row, (128, T)))

    reads = [
        pltpu.make_async_copy(src, dst, io.at[a])
        for a, (src, dst) in enumerate(((hid_in, hid), (tgt_in, tgt), (keep_in, keep), (w_in, w)))
    ]
    for read in reads:
        read.start()

    barrier = pltpu.get_barrier_semaphore()

    def greet_vocab(s):
        pl.semaphore_signal(barrier, inc=1, device_id={"dp": k, "vocab": turn(s + 1, j, nv)}, device_id_type=MESH)

    def greet_dp(s):
        pl.semaphore_signal(barrier, inc=1, device_id={"dp": turn(s + 1, k, n), "vocab": j}, device_id_type=MESH)

    each(nv - 1, greet_vocab)
    each(n - 1, greet_dp)
    for read in reads[:3]:
        read.wait()
    pl.semaphore_wait(barrier, nv + n - 2)

    line = nz == 4
    half = z // 2

    def flip(b):
        return b + half * (3 - 2 * b)

    lead = flip(z)

    def gather(h):
        piece = hid.at[pl.ds(h * Tc, Tc)]
        gat[z, h] = hid[h * Tc:(h + 1) * Tc, :]

        def send(to):
            push(piece, gat.at[z, h], h1_s, h1_r.at[z, h], k, to * cpc + c)

        if line:
            send(flip(3 - lead))
            send(flip(2 - 2 * lead))

            @pl.when(lead == 0)
            def _():
                send(flip(1))
        else:
            each(nz - 1, lambda s: send(turn(s + 1, z, nz)))

    for h in range(min(nc, 2)):
        gather(h)
    if line:

        @pl.when(lead == 0)
        def _():
            g2[flip(3)] = jnp.zeros((nc, Tc, F), bf16)

    tcol[...] = to_wide(tgt[...].astype(f32)).astype(jnp.int32) - j * V
    kcol[...] = to_wide(keep[...].astype(f32)) * loss_scale

    def exchange(h):
        def one(b):
            i, bl = b // zpd, (b % zpd) * cpc + c
            src, dst = gat.at[b, h], hb.at[bl, h, k]

            @pl.when(i != k)
            def _():
                push(src, dst, h2_s, h2_r.at[h], i, j)

            @pl.when(i == k)
            def _():
                hb[bl, h, k] = gat[b, h]

        if line:
            one(z)
            b = flip(1 + lead)
            arrived(gat.at[b, h], h1_r.at[b, h])

            @pl.when(lead == 1)
            def _():
                push(gat.at[b, h], gat.at[b, h], h1_s, h1_r.at[b, h], k, flip(0) * cpc + c)

            one(b)
            for b in (flip(3 - 3 * lead), flip(2 + lead)):
                arrived(gat.at[b, h], h1_r.at[b, h])
                one(b)
        else:
            one(z)

            def rest(s):
                b = turn(s + 1, z, nz)
                arrived(gat.at[b, h], h1_r.at[b, h])
                one(b)

            each(nz - 1, rest)
        if h + 2 < nc:
            gather(h + 2)

    def swap(h):
        if n > 1:
            arrived(hb.at[pl.ds(0, zpd), h, pl.ds(0, n - 1)], h2_r.at[h])
        for d in range(1, cpc):
            for q in range(zpd):
                slot = hb.at[q * cpc + c, h]
                push(slot, slot, h3_s, h3_r.at[h], k, z * cpc + turn(d, c, cpc))

    def partial(h):
        total = None
        for q in range(zpd):
            term = dot_nt(hb[q * cpc + c, h].reshape(n * Tc, F), columns(q, c))
            total = term if total is None else total + term
        if cpc > 1:
            arrived(hb.at[pl.ds(0, (cpc - 1) * zpd), h], h3_r.at[h])
        for d in range(1, cpc):
            for q in range(zpd):
                other = turn(d, c, cpc)
                total += dot_nt(hb[q * cpc + other, h].reshape(n * Tc, F), columns(q, other))
        lp[h] = total.reshape(n, Tc, V)
        for s in range(1, n):
            t = turn(s, k, n)
            push(lp.at[h, t], lr.at[h, s - 1], l_s, l_r.at[h], t, j)

    def hot(h):
        return lax.broadcasted_iota(jnp.int32, (Tc, V), 1) == tcol[h * Tc:(h + 1) * Tc, :1]

    def statistics(h):
        own = lp[h, k]
        if n > 1:
            arrived(lr.at[h], l_r.at[h])
        for s in range(n - 1):
            own += lr[h, s]
        lg[h] = own
        top = jnp.max(own, axis=1, keepdims=True)
        part = jnp.sum(jnp.exp(own - top), axis=1, keepdims=True)
        hit = jnp.sum(jnp.where(hot(h), own, 0.0), axis=1, keepdims=True)
        lane = lax.broadcasted_iota(jnp.int32, (Tc, 128), 1)
        packed = [jnp.where(lane == 0, top, jnp.where(lane == 1, part, hit))]
        if h:
            packed.insert(0, jnp.zeros((h * Tc, 128), f32))
        if h + 1 < nc:
            packed.append(jnp.zeros(((nc - 1 - h) * Tc, 128), f32))
        mine = jnp.transpose(jnp.concatenate(packed, axis=0))[:8, :]
        st[h] = mine
        sr[h, j] = mine

        def tell(s):
            push(st.at[h], sr.at[h, j], s_s, s_r.at[h], k, turn(s + 1, j, nv))

        each(nv - 1, tell)

    def logit_grads(h):
        arrived(sr.at[h, pl.ds(0, nv - 1)], s_r.at[h])
        stats = sr[h]
        tops, parts, hits = stats[:, 0, :], stats[:, 1, :], stats[:, 2, :]
        row_top = jnp.max(tops, axis=0, keepdims=True)
        exp_sum = jnp.sum(parts * jnp.exp(tops - row_top), axis=0, keepdims=True)
        target_logit = jnp.sum(hits, axis=0, keepdims=True)
        log_total = row_top + jnp.log(exp_sum)
        loss = keep[...].astype(f32) * (log_total - target_logit)
        if h:
            lane = lax.broadcasted_iota(jnp.int32, (1, T), 1)
            loss = jnp.where(lane >= h * Tc, loss, loss_out[...])
        loss_out[...] = loss
        soft = jnp.exp(lg[h] - to_wide(log_total)[h * Tc:(h + 1) * Tc, :1])
        scale = kcol[h * Tc:(h + 1) * Tc, :1]
        dall[h, k] = (scale * (soft - jnp.where(hot(h), 1.0, 0.0))).astype(bf16)
        src = dall.at[h, k]
        for s in range(1, n):
            push(src, src, d_s, d_r.at[h], turn(s, k, n), j)

    def other_part(h):
        if n > 1:
            arrived(dall.at[h, pl.ds(0, n - 1)], d_r.at[h])
        rows = dall[h].reshape(n * Tc, V)
        for d in range(1, cpc):
            other = turn(d, c, cpc)
            for q in range(zpd):
                ps[h, d - 1, q] = dot_nn(rows, columns(q, other))
            push(ps.at[h, d - 1], pr.at[h, d - 1], p_s, p_r.at[h], k, z * cpc + other)

    def relay(src, i, q, h):
        to = i * zpd + q
        dst = g2.at[z, h]
        far = flip(to) == 3 if line else False

        def forward():
            @pl.when(to == z)
            def _():
                g2[z, h] = src[...]

            @pl.when(to != z)
            def _():
                sem = g2_r.at[h]
                if not line:
                    push(src, dst, g2_s, sem, k, to * cpc + c)
                    return

                beyond = (lead == 0) & (flip(to) == 2)

                @pl.when(beyond)
                def _():
                    push(src, dst, g2_s, g3_r.at[h], k, to * cpc + c)

                @pl.when(jnp.logical_not(beyond))
                def _():
                    push(src, dst, g2_s, sem, k, to * cpc + c)

        if not line:
            forward()
            return
        pl.when(jnp.logical_not(far))(forward)

        @pl.when(far & (lead == 0))
        def _():
            push(src, via.at[h], g2_s, via_r.at[h], k, flip(1) * cpc + c)

        @pl.when(far & (lead == 1))
        def _():
            mid[h] = src[...]

    def combine(h):
        if not line:
            return

        @pl.when(lead == 1)
        def _():
            arrived(via.at[h], via_r.at[h])
            mid[h] = (mid[h].astype(f32) + via[h].astype(f32)).astype(bf16)
            push(mid.at[h], g2.at[z, h], g2_s, g2_r.at[h], k, flip(3) * cpc + c)

    def own_part(h):
        rows = dall[h].reshape(n * Tc, V)
        for q in range(zpd):
            part_sum = dot_nn(rows, columns(q, c))
            for d in range(1, cpc):
                if q == 0 and d == 1:
                    arrived(pr.at[h], p_r.at[h])
                part_sum += pr[h, d - 1, q]
            gs[h, :, q] = part_sum.astype(bf16).reshape(n, Tc, F)
        for s in range(1, n):
            t = turn(s, k, n)
            push(gs.at[h, t], g1.at[k, h], g1_s, g1_r.at[k, h], t, j)
        for q in range(zpd):
            relay(gs.at[h, k, q], k, q, h)

    def pass_on(h):
        for s in range(1, n):
            i = turn(s, k, n)
            arrived(g1.at[i, h], g1_r.at[i, h])
            for q in range(zpd):
                relay(g1.at[i, h, q], i, q, h)

    def collect(h):
        def take(src):
            return g2[src, h].astype(f32)

        if line:
            arrived(g2.at[pl.ds(0, 2), h], g2_r.at[h])

            @pl.when(lead == 1)
            def _():
                arrived(g2.at[0, h], g3_r.at[h])

            total = take(z) + take(flip(1 - lead)) + take(flip(2)) + take(flip(3))
        else:
            arrived(g2.at[pl.ds(0, nz - 1), h], g2_r.at[h])
            if nz <= 16:
                total = take(0)
                for src in range(1, nz):
                    total += take(src)
            else:
                total = lax.fori_loop(0, nz, lambda s, acc: acc + take(s), jnp.zeros((Tc, F), f32))
        hg_out[h * Tc:(h + 1) * Tc, :] = total.astype(bf16)
        return jnp.sum(total * total)

    def run(stage, h):
        return stage(h)

    for step in range(nc + 5):
        if step < nc:
            run(exchange, step)
        if 0 <= step - 4 < nc:
            run(other_part, step - 4)
        if 0 <= step - 1 < nc:
            run(swap, step - 1)
        if 0 <= step - 3 < nc:
            run(logit_grads, step - 3)
        if 0 <= step - 1 < nc:
            if step == 1:
                reads[3].wait()
            run(partial, step - 1)
        if 0 <= step - 4 < nc:
            run(own_part, step - 4)
        if 0 <= step - 2 < nc:
            run(statistics, step - 2)
        if 0 <= step - 5 < nc - 1:
            run(pass_on, step - 5)
            run(combine, step - 5)

    grads = jnp.transpose(dall[...].reshape(n * T, V))
    squares = jnp.zeros((1, F), f32)
    for bl in range(bpd):
        if bl == bpd // 2:
            run(pass_on, nc - 1)
            run(combine, nc - 1)
        grad = dot_nn(grads, hb[bl].reshape(n * T, F))
        wg_out[:, bl * F:(bl + 1) * F] = grad.astype(bf16)
        squares += jnp.sum(grad * grad, axis=0, keepdims=True)

    both = jnp.sum(squares)
    for h in range(nc):
        both += run(collect, h)

    peers = n * nv
    me = k * nv + j
    n1[me] = jnp.full((1, 128), both, f32)

    def tell_all(s):
        to = turn(s + 1, me, peers)
        push(n1.at[me], n1.at[me], n_s, n_r, to // nv, to % nv)

    each(peers - 1, tell_all)
    arrived(n1.at[pl.ds(0, peers - 1)], n_r)
    norm_out[...] = jnp.sqrt(jnp.sum(n1[...], axis=0))[:, :1]

    arrived(gat.at[pl.ds(0, nz - 1)], h1_s)
    arrived(g2.at[pl.ds(0, nz - 1)], g2_s)
    arrived(sr.at[:, pl.ds(0, nv - 1)], s_s)
    arrived(n1.at[pl.ds(0, peers - 1)], n_s)
    if n > 1:
        arrived(gat.at[pl.ds(0, nz - zpd)], h2_s)
        arrived(lr, l_s)
        arrived(dall.at[:, pl.ds(0, n - 1)], d_s)
        arrived(g1.at[pl.ds(0, n - 1)], g1_s)
    if cpc > 1:
        arrived(hb.at[pl.ds(0, (cpc - 1) * zpd)], h3_s)
        arrived(ps, p_s)


def pad(size, unit):
    return -(-size // unit) * unit


def store(*refs):
    sems = refs[-1]
    copies = [pltpu.make_async_copy(refs[a], refs[a + 4], sems.at[a]) for a in (1, 0, 2, 3)]
    for copy in copies:
        copy.start()
    for copy in copies:
        copy.wait()


def on_device(n, nv, hidden, weight, targets, loss_mask):
    T, F = hidden.shape
    R, V = weight.shape
    bpd = nv // n
    cpc = 2 if bpd % 2 == 0 else 1
    zpd, nz = bpd // cpc, nv // cpc
    nc = 4 if T % 64 == 0 else 1
    Tc = T // nc
    dma = pltpu.SemaphoreType.DMA
    vmem = pl.BlockSpec(memory_space=pltpu.VMEM)
    hbm = pl.BlockSpec(memory_space=pltpu.HBM)
    others = max(cpc - 1, 1)
    kept = 2 * (pad(V, 8) * pad(R, 128) + pad(T, 16) * pad(F, 128)) + 4 * (pad(T, 128) + 128)
    results = pl.pallas_call(
        functools.partial(kernel, n, nv, cpc, nc),
        out_shape=(
            pltpu.VMEM((T, F), bf16),
            pltpu.VMEM((V, R), bf16),
            pltpu.VMEM((1, T), f32),
            pltpu.VMEM((1, 1), f32),
        ),
        in_specs=[hbm] * 4,
        out_specs=(vmem, vmem, vmem, vmem),
        scratch_shapes=[
            pltpu.VMEM((T, F), bf16),
            pltpu.VMEM((1, T), jnp.int32),
            pltpu.VMEM((1, T), jnp.int32),
            pltpu.VMEM((V, R), bf16),
            pltpu.VMEM((nz, nc, Tc, F), bf16),
            pltpu.VMEM((bpd, nc, n, Tc, F), bf16),
            pltpu.VMEM((nc, n, Tc, V), f32),
            pltpu.VMEM((nc, n - 1, Tc, V), f32),
            pltpu.VMEM((nc, Tc, V), f32),
            pltpu.VMEM((T, 128), jnp.int32),
            pltpu.VMEM((T, 128), f32),
            pltpu.VMEM((nc, 8, T), f32),
            pltpu.VMEM((nc, nv, 8, T), f32),
            pltpu.VMEM((nc, n, Tc, V), bf16),
            pltpu.VMEM((nc, others, zpd, n * Tc, F), f32),
            pltpu.VMEM((nc, others, zpd, n * Tc, F), f32),
            pltpu.VMEM((nc, n, zpd, Tc, F), bf16),
            pltpu.VMEM((n, nc, zpd, Tc, F), bf16),
            pltpu.VMEM((nz, nc, Tc, F), bf16),
            pltpu.VMEM((nc, Tc, F), bf16),
            pltpu.VMEM((nc, Tc, F), bf16),
            pltpu.VMEM((n * nv, 1, 128), f32),
            dma((4,)), dma, dma((nz, nc)), dma, dma((nc,)), dma, dma((nc,)), dma, dma((nc,)), dma, dma((nc,)), dma, dma((nc,)),
            dma, dma((nc,)), dma, dma((n, nc)), dma, dma((nc,)), dma((nc,)), dma((nc,)), dma, dma,
        ],
        compiler_params=pltpu.CompilerParams(
            collective_id=0, has_side_effects=True, vmem_limit_bytes=vmem_bytes - kept - 8192
        ),
    )(hidden, weight.T, targets.reshape(1, T), loss_mask.reshape(1, T))
    hg, wg, loss, norm = pl.pallas_call(
        store,
        out_shape=tuple(jax.ShapeDtypeStruct(r.shape, r.dtype) for r in results),
        in_specs=[pl.BlockSpec(memory_space=pl.ANY)] * 4,
        out_specs=(hbm,) * 4,
        scratch_shapes=[dma((4,))],
        compiler_params=pltpu.CompilerParams(vmem_limit_bytes=1024 * 1024),
    )(*results)
    return hg, wg.T, loss.reshape(T), norm.reshape(())


def solution(mesh):
    placed = (P("dp", "vocab"), P("dp", "vocab"), P("dp"), P("dp"))
    return jax.shard_map(
        functools.partial(on_device, mesh.shape["dp"], mesh.shape["vocab"]),
        mesh=mesh,
        in_specs=placed,
        out_specs=(P("dp", "vocab"), P("dp", "vocab"), P("dp"), P()),
        check_vma=False,
    )
```

time: 114 us -> 84.1 us (0.74)
  Pallas kernels: 106 us -> 83.3 us
  local copies, waits for them, and re-layouts: 6.81 us -> 0 us
    pallas_call x1 -> x2, Pallas kernels: 106 us -> 83.3 us  [the longest x1 81.1 us: on_device(): pl.pallas_call(functools.partial(kernel, n, nv, cpc, nc), out_shape=(pltp...]
    unnamed x5 -> x0, local copies, waits for them, and re-layouts: 5.62 us -> none
    slice x1 -> x0, local copies, waits for them, and re-layouts: 1.19 us -> none  [on_device(): return (hg, wg.T, loss.reshape(T), norm[0, 0])]
where the time goes in v1:
time: 84.1 us; the launch traced here: 83.9 us
  Pallas kernels  83.3 us (99%)
    pallas_call x1, Pallas kernels, on_device(): pl.pallas_call(functools.partial(kernel, n, nv, cpc, nc), out_shape=(pltp...  81.1 us
    pallas_call x1, Pallas kernels, on_device(): pl.pallas_call(store, out_shape=tuple((jax.ShapeDtypeStruct(r.shape, r.dt...  2.18 us

profile of v1, /device:TPU:0, one launch (start us, length us, event | category | flops | bytes accessed | tf_op | source)
XLA Modules:
  0.0 83.9 jit_solution(3238065435407354975)
XLA Ops:
  0.6 81.1 %shard_map.75 = (bf16[128,1024]{1,0:T(8,128)(2,1)S(1)}, bf16[594,2048]{1,0:T(8,128)(2,1)S(1)}, f32[1,128]{1,0:T(1,128)S(1)}, f32[1,1]{1,0:T(1,128)}) custom-call(bf16[128,1024]{1,0:T(8,128)(2,1)} %hid_in.1, bf16[594,2048]{1,0:T(8,128)(2,1)} %bitcast.6, s32[1,128]{1,0:T(1,128)} %bitcast.7, s32[1,128]{1,0:T(1,128)} %bitcast.8), custom_call_target="tpu_custom_call" | custom-call | tf_op jit(solution)/shard_map/pallas_call | solution.py:441
  81.7 2.2 %shard_map.76 = (bf16[128,1024]{1,0:T(8,128)(2,1)}, bf16[594,2048]{1,0:T(8,128)(2,1)}, f32[1,128]{1,0:T(1,128)}, f32[1,1]{1,0:T(1,128)}) custom-call(bf16[128,1024]{1,0:T(8,128)(2,1)S(1)} %get-tuple-element.12.refs_0_, bf16[594,2048]{1,0:T(8,128)(2,1)S(1)} %get-tuple-element.13.refs_1_, f32[1,128]{1,0:T(1,128)S(1)} %get-tuple-element.14.refs_2_, ...), custom_call_target="tpu_custom_call" | custom-call | tf_op jit(solution)/shard_map/pallas_call | solution.py:481

commit v2 on v1

v2 whole, which is shorter than its diff:
```python
import functools
import math

import jax
import jax.numpy as jnp
from jax import lax
from jax.experimental import pallas as pl
from jax.experimental.pallas import tpu as pltpu
from jax.sharding import PartitionSpec as P

loss_scale = 16.0
MESH = pl.DeviceIdType.MESH
f32 = jnp.float32
bf16 = jnp.bfloat16
vmem_bytes = 67043328


def dot_nn(a, b):
    return jnp.dot(a, b, preferred_element_type=f32)


def each(count, body):
    if count <= 32:
        for s in range(count):
            body(s)
    else:

        def step(s, carry):
            body(s)
            return carry

        lax.fori_loop(0, count, step, 0)


def kernel(
    n, nv, cpc, sizes,
    hid_in, w_in, tgt_in, keep_in,
    hg_out, wg_out, loss_out, norm_out,
    hid, tgt, keep, w, wt, gat, hb, lp, lr, lg, tcol, kcol, st, sr, dall, ps, pr, gs, g1, g2, via, mid, gt, n1,
    io, h1_s, h1_r, h2_s, h2_r, h3_s, h3_r, l_s, l_r, s_s, s_r, d_s, d_r,
    p_s, p_r, g1_s, g1_r, g2_s, g2_r, g3_r, via_r, n_s, n_r,
):
    T, F = hid.shape
    V = w.shape[0]
    nc = len(sizes)
    starts = [sum(sizes[:h]) for h in range(nc)]
    unit = math.gcd(*sizes)
    bpd = nv // n
    zpd = bpd // cpc
    nz = nv // cpc
    k = lax.axis_index("dp")
    j = lax.axis_index("vocab")
    z, c = j // cpc, j % cpc

    def push(src, dst, ss, rs, dp, vocab):
        pltpu.make_async_remote_copy(
            src_ref=src, dst_ref=dst, send_sem=ss, recv_sem=rs,
            device_id={"dp": dp, "vocab": vocab}, device_id_type=MESH,
        ).start()

    def arrived(dst, sem):
        pltpu.make_async_copy(dst, dst, sem).wait()

    def peer(s):
        return (n - 1 - k, k + 1 - 2 * (k % 2), turn(2, k, n))[s - 1] if n == 4 else turn(s, k, n)

    def mine(h):
        return pl.ds(starts[h], sizes[h])

    def every(h):
        return pl.ds(n * starts[h], n * sizes[h])

    def of(t, h):
        return pl.ds(pl.multiple_of(n * starts[h] + t * sizes[h], unit), sizes[h])

    def turn(s, base, size):
        return lax.rem(base + s, size)

    def columns(q, core):
        if F % 128 == 0:
            return w[:, pl.ds(pl.multiple_of((q * cpc + core) * F, F), F)]
        out = w[:, q * cpc * F:(q * cpc + 1) * F]
        for a in range(1, cpc):
            out = jnp.where(core == a, w[:, (q * cpc + a) * F:(q * cpc + a + 1) * F], out)
        return out

    def rows_of(q, core):
        return wt[pl.ds(pl.multiple_of((q * cpc + core) * F, F), F), :]

    def to_wide(row):
        return jnp.transpose(jnp.broadcast_to(row, (128, T)))

    reads = [
        pltpu.make_async_copy(src, dst, io.at[a])
        for a, (src, dst) in enumerate(((hid_in, hid), (tgt_in, tgt), (keep_in, keep), (w_in, w)))
    ]
    for read in reads:
        read.start()

    barrier = pltpu.get_barrier_semaphore()

    def greet_vocab(s):
        pl.semaphore_signal(barrier, inc=1, device_id={"dp": k, "vocab": turn(s + 1, j, nv)}, device_id_type=MESH)

    def greet_dp(s):
        pl.semaphore_signal(barrier, inc=1, device_id={"dp": turn(s + 1, k, n), "vocab": j}, device_id_type=MESH)

    each(nv - 1, greet_vocab)
    each(n - 1, greet_dp)
    for read in reads[:3]:
        read.wait()
    pl.semaphore_wait(barrier, nv + n - 2)

    line = nz == 4
    half = z // 2

    def flip(b):
        return b + half * (3 - 2 * b)

    lead = flip(z)

    def gather(h):
        piece = hid.at[mine(h)]
        gat[z, mine(h), :] = hid[mine(h), :]

        def send(to):
            push(piece, gat.at[z, mine(h)], h1_s, h1_r.at[z, h], k, to * cpc + c)

        if line:
            send(flip(3 - lead))
            send(flip(2 - 2 * lead))

            @pl.when(lead == 0)
            def _():
                send(flip(1))
        else:
            each(nz - 1, lambda s: send(turn(s + 1, z, nz)))

    for h in range(min(nc, 2)):
        gather(h)
    if line:

        @pl.when(lead == 0)
        def _():
            g2[flip(3)] = jnp.zeros((T, F), bf16)

    reads[3].wait()
    wt[...] = jnp.transpose(w[...])
    tcol[...] = to_wide(tgt[...].astype(f32)).astype(jnp.int32) - j * V
    kcol[...] = to_wide(keep[...].astype(f32)) * loss_scale

    def exchange(h):
        def one(b):
            i, bl = b // zpd, (b % zpd) * cpc + c
            src, dst = gat.at[b, mine(h)], hb.at[bl, of(k, h)]

            @pl.when(i != k)
            def _():
                push(src, dst, h2_s, h2_r.at[h], i, j)

            @pl.when(i == k)
            def _():
                hb[bl, of(k, h), :] = gat[b, mine(h), :]

        if line:
            one(z)
            b = flip(1 + lead)
            arrived(gat.at[b, mine(h)], h1_r.at[b, h])

            @pl.when(lead == 1)
            def _():
                push(gat.at[b, mine(h)], gat.at[b, mine(h)], h1_s, h1_r.at[b, h], k, flip(0) * cpc + c)

            one(b)
            for b in (flip(3 - 3 * lead), flip(2 + lead)):
                arrived(gat.at[b, mine(h)], h1_r.at[b, h])
                one(b)
        else:
            one(z)

            def rest(s):
                b = turn(s + 1, z, nz)
                arrived(gat.at[b, mine(h)], h1_r.at[b, h])
                one(b)

            each(nz - 1, rest)
        if h + 2 < nc:
            gather(h + 2)

    def swap(h):
        if n > 1:
            arrived(hb.at[pl.ds(0, zpd), pl.ds(0, (n - 1) * sizes[h])], h2_r.at[h])
        for d in range(1, cpc):
            for q in range(zpd):
                slot = hb.at[q * cpc + c, every(h)]
                push(slot, slot, h3_s, h3_r.at[h], k, z * cpc + turn(d, c, cpc))

    def theirs(s, h):
        return pl.ds((n - 1) * starts[h] + (s - 1) * sizes[h], sizes[h])

    def partial(h):
        total = None
        for q in range(zpd):
            term = dot_nn(hb[q * cpc + c, every(h), :], rows_of(q, c))
            total = term if total is None else total + term
        if cpc > 1:
            arrived(hb.at[pl.ds(0, (cpc - 1) * zpd), every(h)], h3_r.at[h])
        for d in range(1, cpc):
            for q in range(zpd):
                other = turn(d, c, cpc)
                total += dot_nn(hb[q * cpc + other, every(h), :], rows_of(q, other))
        lp[every(h), :] = total
        for s in range(1, n):
            t = peer(s)
            push(lp.at[of(t, h)], lr.at[theirs(s, h)], l_s, l_r.at[h], t, j)

    def hot(h):
        return lax.broadcasted_iota(jnp.int32, (sizes[h], V), 1) == tcol[mine(h), :][:, :1]

    def statistics(h):
        own = lp[of(k, h), :]
        if n > 1:
            arrived(lr.at[pl.ds(0, (n - 1) * sizes[h])], l_r.at[h])
        for s in range(1, n):
            own += lr[theirs(s, h), :]
        lg[mine(h), :] = own
        top = jnp.max(own, axis=1, keepdims=True)
        part = jnp.sum(jnp.exp(own - top), axis=1, keepdims=True)
        hit = jnp.sum(jnp.where(hot(h), own, 0.0), axis=1, keepdims=True)
        lane = lax.broadcasted_iota(jnp.int32, (sizes[h], 128), 1)
        packed = [jnp.where(lane == 0, top, jnp.where(lane == 1, part, hit))]
        if h:
            packed.insert(0, jnp.zeros((starts[h], 128), f32))
        if h + 1 < nc:
            packed.append(jnp.zeros((T - starts[h] - sizes[h], 128), f32))
        told = jnp.transpose(jnp.concatenate(packed, axis=0))[:8, :]
        st[h] = told
        sr[h, j] = told

        def tell(s):
            push(st.at[h], sr.at[h, j], s_s, s_r.at[h], k, turn(s + 1, j, nv))

        each(nv - 1, tell)

    def logit_grads(h):
        arrived(sr.at[h, pl.ds(0, nv - 1)], s_r.at[h])
        stats = sr[h]
        tops, parts, hits = stats[:, 0, :], stats[:, 1, :], stats[:, 2, :]
        row_top = jnp.max(tops, axis=0, keepdims=True)
        exp_sum = jnp.sum(parts * jnp.exp(tops - row_top), axis=0, keepdims=True)
        target_logit = jnp.sum(hits, axis=0, keepdims=True)
        log_total = row_top + jnp.log(exp_sum)
        loss = keep[...].astype(f32) * (log_total - target_logit)
        if h:
            lane = lax.broadcasted_iota(jnp.int32, (1, T), 1)
            loss = jnp.where(lane >= starts[h], loss, loss_out[...])
        loss_out[...] = loss
        soft = jnp.exp(lg[mine(h), :] - to_wide(log_total)[starts[h]:starts[h] + sizes[h], :1])
        scale = kcol[mine(h), :][:, :1]
        dall[of(k, h), :] = (scale * (soft - jnp.where(hot(h), 1.0, 0.0))).astype(bf16)
        src = dall.at[of(k, h)]
        for s in range(1, n):
            push(src, src, d_s, d_r.at[h], peer(s), j)

    def other_part(h):
        if n > 1:
            arrived(dall.at[pl.ds(0, (n - 1) * sizes[h])], d_r.at[h])
        rows = dall[every(h), :]
        for d in range(1, cpc):
            other = turn(d, c, cpc)
            for q in range(zpd):
                ps[d - 1, q, every(h), :] = dot_nn(rows, columns(q, other))
            push(ps.at[d - 1, :, every(h)], pr.at[d - 1, :, every(h)], p_s, p_r.at[h], k, z * cpc + other)

    def relay(src, i, q, h):
        to = i * zpd + q
        dst = g2.at[z, mine(h)]
        far = flip(to) == 3 if line else False

        def forward():
            @pl.when(to == z)
            def _():
                g2[z, mine(h), :] = src[...]

            @pl.when(to != z)
            def _():
                sem = g2_r.at[h]
                if not line:
                    push(src, dst, g2_s, sem, k, to * cpc + c)
                    return

                beyond = (lead == 0) & (flip(to) == 2)

                @pl.when(beyond)
                def _():
                    push(src, dst, g2_s, g3_r.at[h], k, to * cpc + c)

                @pl.when(jnp.logical_not(beyond))
                def _():
                    push(src, dst, g2_s, sem, k, to * cpc + c)

        if not line:
            forward()
            return
        pl.when(jnp.logical_not(far))(forward)

        @pl.when(far & (lead == 0))
        def _():
            push(src, via.at[mine(h)], g2_s, via_r.at[h], k, flip(1) * cpc + c)

        @pl.when(far & (lead == 1))
        def _():
            mid[mine(h), :] = src[...]

    def combine(h):
        if not line:
            return

        @pl.when(lead == 1)
        def _():
            arrived(via.at[mine(h)], via_r.at[h])
            mid[mine(h), :] = (mid[mine(h), :].astype(f32) + via[mine(h), :].astype(f32)).astype(bf16)
            push(mid.at[mine(h)], g2.at[z, mine(h)], g2_s, g2_r.at[h], k, flip(3) * cpc + c)

    def own_part(h):
        rows = dall[every(h), :]
        for q in range(zpd):
            part_sum = dot_nn(rows, columns(q, c))
            for d in range(1, cpc):
                if q == 0 and d == 1:
                    arrived(pr.at[:, :, every(h)], p_r.at[h])
                part_sum += pr[d - 1, q, every(h), :]
            gs[q, every(h), :] = part_sum.astype(bf16)
        for s in range(1, n):
            t = peer(s)
            push(gs.at[:, of(t, h)], g1.at[k, :, mine(h)], g1_s, g1_r.at[k, h], t, j)
        for q in range(zpd):
            relay(gs.at[q, of(k, h)], k, q, h)

    def pass_on(h):
        def one(i):
            arrived(g1.at[i, :, mine(h)], g1_r.at[i, h])
            for q in range(zpd):
                relay(g1.at[i, q, mine(h)], i, q, h)

        if line:
            for d in (3, 2, 1, 0):
                i = flip(d)
                pl.when(i != k)(functools.partial(one, i))
        else:
            for s in range(1, n):
                one(turn(s, k, n))

    def collect(h):
        def take(src):
            return g2[src, mine(h), :].astype(f32)

        if line:
            arrived(g2.at[pl.ds(0, 2), mine(h)], g2_r.at[h])

            @pl.when(lead == 1)
            def _():
                arrived(g2.at[0, mine(h)], g3_r.at[h])

            total = take(z) + take(flip(1 - lead)) + take(flip(2)) + take(flip(3))
        else:
            arrived(g2.at[pl.ds(0, nz - 1), mine(h)], g2_r.at[h])
            if nz <= 16:
                total = take(0)
                for src in range(1, nz):
                    total += take(src)
            else:
                total = lax.fori_loop(0, nz, lambda s, acc: acc + take(s), jnp.zeros((sizes[h], F), f32))
        hg_out[mine(h), :] = total.astype(bf16)
        sums.append(jnp.sum(total * total))

    def run(stage, h):
        return stage(h)

    def weight_grad(bl):
        if bl == 0:
            gt[...] = jnp.transpose(dall[...])
        grad = dot_nn(gt[...], hb[bl])
        wg_out[:, bl * F:(bl + 1) * F] = grad.astype(bf16)
        sums.append(jnp.sum(grad * grad))

    sums = []
    plan = [(at + gap * (4 * (starts[h] + sizes[h]) / T - 1), stage, h) for stage, at, gap in (
        (exchange, 8, 4), (swap, 12.5, 4), (partial, 13, 4), (statistics, 18.5, 4), (logit_grads, 22, 4), (other_part, 26, 4),
        (own_part, 28, 4), (pass_on, 33, 4), (combine, 38, 4), (collect, 60, 1),
    ) for h in range(nc)]
    plan += [(43 + 16 * bl / bpd, weight_grad, bl) for bl in range(bpd)]
    for _, stage, h in sorted(plan, key=lambda entry: entry[0]):
        run(stage, h)

    both = sum(sums)

    peers = n * nv
    me = k * nv + j
    n1[me] = jnp.full((1, 128), both, f32)

    def tell_all(s):
        to = turn(s + 1, me, peers)
        push(n1.at[me], n1.at[me], n_s, n_r, to // nv, to % nv)

    each(peers - 1, tell_all)
    arrived(n1.at[pl.ds(0, peers - 1)], n_r)
    norm_out[...] = jnp.sqrt(jnp.sum(n1[...], axis=0))[:, :1]

    arrived(gat.at[pl.ds(0, nz - 1)], h1_s)
    arrived(g2.at[pl.ds(0, nz - 1)], g2_s)
    arrived(sr.at[:, pl.ds(0, nv - 1)], s_s)
    arrived(n1.at[pl.ds(0, peers - 1)], n_s)
    if n > 1:
        arrived(gat.at[pl.ds(0, nz - zpd)], h2_s)
        arrived(lr, l_s)
        arrived(dall.at[pl.ds(0, (n - 1) * T)], d_s)
        arrived(g1.at[pl.ds(0, n - 1)], g1_s)
    if cpc > 1:
        arrived(hb.at[pl.ds(0, (cpc - 1) * zpd)], h3_s)
        arrived(ps, p_s)


def pad(size, unit):
    return -(-size // unit) * unit


def store(*refs):
    sems = refs[-1]
    copies = [pltpu.make_async_copy(refs[a], refs[a + 4], sems.at[a]) for a in (1, 0, 2, 3)]
    for copy in copies:
        copy.start()
    for copy in copies:
        copy.wait()


def on_device(n, nv, hidden, weight, targets, loss_mask):
    T, F = hidden.shape
    R, V = weight.shape
    bpd = nv // n
    cpc = 2 if bpd % 2 == 0 else 1
    zpd, nz = bpd // cpc, nv // cpc
    sizes = [T // 8 * part for part in (1, 1, 2, 2, 1, 1)] if T % 128 == 0 else [T]
    nc = len(sizes)
    dma = pltpu.SemaphoreType.DMA
    vmem = pl.BlockSpec(memory_space=pltpu.VMEM)
    hbm = pl.BlockSpec(memory_space=pltpu.HBM)
    others = max(cpc - 1, 1)
    kept = 2 * (pad(V, 8) * pad(R, 128) + pad(T, 16) * pad(F, 128)) + 4 * (pad(T, 128) + 128)
    results = pl.pallas_call(
        functools.partial(kernel, n, nv, cpc, sizes),
        out_shape=(
            pltpu.VMEM((T, F), bf16),
            pltpu.VMEM((V, R), bf16),
            pltpu.VMEM((1, T), f32),
            pltpu.VMEM((1, 1), f32),
        ),
        in_specs=[hbm] * 4,
        out_specs=(vmem, vmem, vmem, vmem),
        scratch_shapes=[
            pltpu.VMEM((T, F), bf16),
            pltpu.VMEM((1, T), jnp.int32),
            pltpu.VMEM((1, T), jnp.int32),
            pltpu.VMEM((V, R), bf16),
            pltpu.VMEM((R, V), bf16),
            pltpu.VMEM((nz, T, F), bf16),
            pltpu.VMEM((bpd, n * T, F), bf16),
            pltpu.VMEM((n * T, V), f32),
            pltpu.VMEM((max(n - 1, 1) * T, V), f32),
            pltpu.VMEM((T, V), f32),
            pltpu.VMEM((T, 128), jnp.int32),
            pltpu.VMEM((T, 128), f32),
            pltpu.VMEM((nc, 8, T), f32),
            pltpu.VMEM((nc, nv, 8, T), f32),
            pltpu.VMEM((n * T, V), bf16),
            pltpu.VMEM((others, zpd, n * T, F), f32),
            pltpu.VMEM((others, zpd, n * T, F), f32),
            pltpu.VMEM((zpd, n * T, F), bf16),
            pltpu.VMEM((n, zpd, T, F), bf16),
            pltpu.VMEM((nz, T, F), bf16),
            pltpu.VMEM((T, F), bf16),
            pltpu.VMEM((T, F), bf16),
            pltpu.VMEM((V, n * T), bf16),
            pltpu.VMEM((n * nv, 1, 128), f32),
            dma((4,)), dma, dma((nz, nc)), dma, dma((nc,)), dma, dma((nc,)), dma, dma((nc,)), dma, dma((nc,)), dma, dma((nc,)),
            dma, dma((nc,)), dma, dma((n, nc)), dma, dma((nc,)), dma((nc,)), dma((nc,)), dma, dma,
        ],
        compiler_params=pltpu.CompilerParams(
            collective_id=0, has_side_effects=True, vmem_limit_bytes=vmem_bytes - kept - 8192
        ),
    )(hidden, weight.T, targets.reshape(1, T), loss_mask.reshape(1, T))
    hg, wg, loss, norm = pl.pallas_call(
        store,
        out_shape=tuple(jax.ShapeDtypeStruct(r.shape, r.dtype) for r in results),
        in_specs=[pl.BlockSpec(memory_space=pl.ANY)] * 4,
        out_specs=(hbm,) * 4,
        scratch_shapes=[dma((4,))],
        compiler_params=pltpu.CompilerParams(vmem_limit_bytes=1024 * 1024),
    )(*results)
    return hg, wg.T, loss.reshape(T), norm.reshape(())


def solution(mesh):
    placed = (P("dp", "vocab"), P("dp", "vocab"), P("dp"), P("dp"))
    return jax.shard_map(
        functools.partial(on_device, mesh.shape["dp"], mesh.shape["vocab"]),
        mesh=mesh,
        in_specs=placed,
        out_specs=(P("dp", "vocab"), P("dp", "vocab"), P("dp"), P()),
        check_vma=False,
    )
```

time: 84.1 us -> 79.7 us (0.948)
  Pallas kernels: 83.3 us -> 78.9 us
    pallas_call x1, Pallas kernels: 81.1 us -> 76.7 us  [on_device(): pl.pallas_call(functools.partial(kernel, n, nv, cpc, sizes), out_shape=(p...]
where the time goes in v2:
time: 79.7 us; the launch traced here: 79.6 us
  Pallas kernels  78.9 us (99%)
    pallas_call x1, Pallas kernels, on_device(): pl.pallas_call(functools.partial(kernel, n, nv, cpc, sizes), out_shape=(p...  76.7 us
    pallas_call x1, Pallas kernels, on_device(): pl.pallas_call(store, out_shape=tuple((jax.ShapeDtypeStruct(r.shape, r.dt...  2.18 us

profile of v2, /device:TPU:0, one launch (start us, length us, event | category | flops | bytes accessed | tf_op | source)
XLA Modules:
  0.0 79.6 jit_solution(10994536399376023557)
XLA Ops:
  0.6 76.7 %shard_map.75 = (bf16[128,1024]{1,0:T(8,128)(2,1)S(1)}, bf16[594,2048]{1,0:T(8,128)(2,1)S(1)}, f32[1,128]{1,0:T(1,128)S(1)}, f32[1,1]{1,0:T(1,128)}) custom-call(bf16[128,1024]{1,0:T(8,128)(2,1)} %hid_in.1, bf16[594,2048]{1,0:T(8,128)(2,1)} %bitcast.6, s32[1,128]{1,0:T(1,128)} %bitcast.7, s32[1,128]{1,0:T(1,128)} %bitcast.8), custom_call_target="tpu_custom_call" | custom-call | tf_op jit(solution)/shard_map/pallas_call | solution.py:450
  77.4 2.2 %shard_map.76 = (bf16[128,1024]{1,0:T(8,128)(2,1)}, bf16[594,2048]{1,0:T(8,128)(2,1)}, f32[1,128]{1,0:T(1,128)}, f32[1,1]{1,0:T(1,128)}) custom-call(bf16[128,1024]{1,0:T(8,128)(2,1)S(1)} %get-tuple-element.12.refs_0_, bf16[594,2048]{1,0:T(8,128)(2,1)S(1)} %get-tuple-element.13.refs_1_, f32[1,128]{1,0:T(1,128)S(1)} %get-tuple-element.14.refs_2_, ...), custom_call_target="tpu_custom_call" | custom-call | tf_op jit(solution)/shard_map/pallas_call | solution.py:492

commit v3 on v2

--- a/solution.py
+++ b/solution.py
@@ -36,7 +36,7 @@
     n, nv, cpc, sizes,
     hid_in, w_in, tgt_in, keep_in,
     hg_out, wg_out, loss_out, norm_out,
-    hid, tgt, keep, w, wt, gat, hb, lp, lr, lg, tcol, kcol, st, sr, dall, ps, pr, gs, g1, g2, via, mid, gt, n1,
+    hid, tgt, keep, w, wt, gat, hb, lp, lr, lg, tcol, kcol, st, sr, dall, ps, pr, gs, g1, g2, via, mid, gt, lx, x_r, n1,
     io, h1_s, h1_r, h2_s, h2_r, h3_s, h3_r, l_s, l_r, s_s, s_r, d_s, d_r,
     p_s, p_r, g1_s, g1_r, g2_s, g2_r, g3_r, via_r, n_s, n_r,
 ):
@@ -64,6 +64,12 @@
     def peer(s):
         return (n - 1 - k, k + 1 - 2 * (k % 2), turn(2, k, n))[s - 1] if n == 4 else turn(s, k, n)
 
+    square = n == 4 and unit % 16 == 0
+
+    def part_of(t, h, a):
+        size = sizes[h] // 2
+        return pl.ds(pl.multiple_of(n * starts[h] + t * sizes[h] + a * size, unit // 2), size)
+
     def mine(h):
         return pl.ds(starts[h], sizes[h])
 
@@ -210,18 +216,39 @@
                 other = turn(d, c, cpc)
                 total += dot_nn(hb[q * cpc + other, every(h), :], rows_of(q, other))
         lp[every(h), :] = total
+        if square:
+            for a in (0, 1):
+                size = sizes[h] // 2
+                push(lp.at[part_of(peer(1), h, a)], lx.at[a, pl.ds(starts[h] // 2, size)], l_s, x_r.at[h], peer(2 + a), j)
+            for a in (0, 1):
+                push(lp.at[part_of(peer(2 + a), h, a)], lr.at[half_of(a, h, a)], l_s, l_r.at[h], peer(2 + a), j)
+            return
         for s in range(1, n):
             t = peer(s)
             push(lp.at[of(t, h)], lr.at[theirs(s, h)], l_s, l_r.at[h], t, j)
 
+    def half_of(s, h, a):
+        size = sizes[h] // 2
+        return pl.ds((n - 1) * starts[h] + s * sizes[h] + a * size, size)
+
+    def across(h):
+        if not square:
+            return
+        size = sizes[h] // 2
+        arrived(lx.at[:, pl.ds(0, size)], x_r.at[h])
+        for a in (0, 1):
+            rows, t = part_of(peer(3 - a), h, a), peer(3 - a)
+            lp[rows, :] = lp[rows, :] + lx[a, pl.ds(starts[h] // 2, size), :]
+            push(lp.at[rows], lr.at[half_of(1 - a, h, a)], l_s, l_r.at[h], t, j)
+
     def hot(h):
         return lax.broadcasted_iota(jnp.int32, (sizes[h], V), 1) == tcol[mine(h), :][:, :1]
 
     def statistics(h):
         own = lp[of(k, h), :]
         if n > 1:
-            arrived(lr.at[pl.ds(0, (n - 1) * sizes[h])], l_r.at[h])
-        for s in range(1, n):
+            arrived(lr.at[pl.ds(0, (2 if square else n - 1) * sizes[h])], l_r.at[h])
+        for s in range(1, 3 if square else n):
             own += lr[theirs(s, h), :]
         lg[mine(h), :] = own
         top = jnp.max(own, axis=1, keepdims=True)
@@ -386,10 +413,10 @@
 
     sums = []
     plan = [(at + gap * (4 * (starts[h] + sizes[h]) / T - 1), stage, h) for stage, at, gap in (
-        (exchange, 8, 4), (swap, 12.5, 4), (partial, 13, 4), (statistics, 18.5, 4), (logit_grads, 22, 4), (other_part, 26, 4),
-        (own_part, 28, 4), (pass_on, 33, 4), (combine, 38, 4), (collect, 60, 1),
+        (exchange, 8, 4), (swap, 12.5, 4), (partial, 13, 4), (across, 16, 4), (statistics, 18.5, 4), (logit_grads, 22.0, 4), (other_part, 26.0, 4),
+        (own_part, 28.0, 4), (pass_on, 33.0, 4), (combine, 38.0, 4), (collect, 44, 4),
     ) for h in range(nc)]
-    plan += [(43 + 16 * bl / bpd, weight_grad, bl) for bl in range(bpd)]
+    plan += [(43 + 3 * bl / bpd, weight_grad, bl) for bl in range(bpd)]
     for _, stage, h in sorted(plan, key=lambda entry: entry[0]):
         run(stage, h)
 
@@ -413,7 +440,7 @@
     arrived(n1.at[pl.ds(0, peers - 1)], n_s)
     if n > 1:
         arrived(gat.at[pl.ds(0, nz - zpd)], h2_s)
-        arrived(lr, l_s)
+        arrived(lp.at[pl.ds(0, (n - 1) * T)], l_s)
         arrived(dall.at[pl.ds(0, (n - 1) * T)], d_s)
         arrived(g1.at[pl.ds(0, n - 1)], g1_s)
     if cpc > 1:
@@ -481,6 +508,8 @@
             pltpu.VMEM((T, F), bf16),
             pltpu.VMEM((T, F), bf16),
             pltpu.VMEM((V, n * T), bf16),
+            pltpu.VMEM((2, max(T // 2, 8), V), f32),
+            dma((nc,)),
             pltpu.VMEM((n * nv, 1, 128), f32),
             dma((4,)), dma, dma((nz, nc)), dma, dma((nc,)), dma, dma((nc,)), dma, dma((nc,)), dma, dma((nc,)), dma, dma((nc,)),
             dma, dma((nc,)), dma, dma((n, nc)), dma, dma((nc,)), dma((nc,)), dma((nc,)), dma, dma,

time: 79.7 us -> 79.4 us (level)
  no operation moved by 1% of the time
where the time goes in v3:
time: 79.4 us; the launch traced here: 79.2 us
  Pallas kernels  78.6 us (99%)
    pallas_call x1, Pallas kernels, on_device(): pl.pallas_call(functools.partial(kernel, n, nv, cpc, sizes), out_shape=(p...  76.4 us
    pallas_call x1, Pallas kernels, on_device(): pl.pallas_call(store, out_shape=tuple((jax.ShapeDtypeStruct(r.shape, r.dt...  2.18 us

profile of v3, /device:TPU:0, one launch (start us, length us, event | category | flops | bytes accessed | tf_op | source)
XLA Modules:
  0.0 79.2 jit_solution(7734051265728254807)
XLA Ops:
  0.6 76.4 %shard_map.75 = (bf16[128,1024]{1,0:T(8,128)(2,1)S(1)}, bf16[594,2048]{1,0:T(8,128)(2,1)S(1)}, f32[1,128]{1,0:T(1,128)S(1)}, f32[1,1]{1,0:T(1,128)}) custom-call(bf16[128,1024]{1,0:T(8,128)(2,1)} %hid_in.1, bf16[594,2048]{1,0:T(8,128)(2,1)} %bitcast.6, s32[1,128]{1,0:T(1,128)} %bitcast.7, s32[1,128]{1,0:T(1,128)} %bitcast.8), custom_call_target="tpu_custom_call" | custom-call | tf_op jit(solution)/shard_map/pallas_call | solution.py:477
  77.0 2.2 %shard_map.76 = (bf16[128,1024]{1,0:T(8,128)(2,1)}, bf16[594,2048]{1,0:T(8,128)(2,1)}, f32[1,128]{1,0:T(1,128)}, f32[1,1]{1,0:T(1,128)}) custom-call(bf16[128,1024]{1,0:T(8,128)(2,1)S(1)} %get-tuple-element.12.refs_0_, bf16[594,2048]{1,0:T(8,128)(2,1)S(1)} %get-tuple-element.13.refs_1_, f32[1,128]{1,0:T(1,128)S(1)} %get-tuple-element.14.refs_2_, ...), custom_call_target="tpu_custom_call" | custom-call | tf_op jit(solution)/shard_map/pallas_call | solution.py:521
